TPU v7x, 32 devices: a whole 2x2x4 slice. The times are simulated.
32 devices in a mesh: shard: 4 (over x, core), replica: 8 (over z, y).
Axes of the slice: x: 2, y: 2, z: 4, core: 2. Of those that a mesh axis runs over, the one named last changes fastest.
Arguments:
- tokens: bfloat16 [16384, 768], P(('shard', 'replica')), may hold values from -6 to 6
- cotangent: bfloat16 [16384, 768], P(('shard', 'replica')), may hold values from -6 to 6
- lengths: int32 [32], replicated, may hold values from 16 to 512, as said below
- assignment: int32 [32], replicated, may hold values from 0 to 31, as said below
- positions: int32 [16384], P(('shard', 'replica')), may hold values from 0 to 2047, as said below
- attention_gain: bfloat16 [768], P('shard'), may hold values from 0.25 to 2.5
- query_weight: bfloat16 [768, 768], P('shard'), may hold values from -0.21875 to 0.21875
- key_weight: bfloat16 [768, 768], P('shard'), may hold values from -0.21875 to 0.21875
- value_weight: bfloat16 [768, 768], P('shard'), may hold values from -0.21875 to 0.21875
- out_weight: bfloat16 [768, 768], P('shard'), may hold values from -1.25 to 1.25
- feedforward_gain: bfloat16 [768], P('shard'), may hold values from 0.25 to 2.5
- gate_weight: bfloat16 [768, 3072], P('shard'), may hold values from -0.21875 to 0.21875
- up_weight: bfloat16 [768, 3072], P('shard'), may hold values from -0.21875 to 0.21875
- down_weight: bfloat16 [3072, 768], P('shard'), may hold values from -0.21875 to 0.21875
Outputs:
- output: bfloat16 [16384, 768], P(('shard', 'replica'))
- input_grad: float32 [16384, 768], P(('shard', 'replica'))
- attention_gain_grad: float32 [768], P('shard')
- query_grad: float32 [768, 768], P('shard')
- key_grad: float32 [768, 768], P('shard')
- value_grad: float32 [768, 768], P('shard')
- out_grad: float32 [768, 768], P('shard')
- feedforward_gain_grad: float32 [768], P('shard')
- gate_grad: float32 [768, 3072], P('shard')
- up_grad: float32 [768, 3072], P('shard')
- down_grad: float32 [3072, 768], P('shard')
Inputs may be any that keep to these rules, and one draw needn't show every extreme that they name: `lengths`: each block holds exactly 1 sequence, 16 to 512 rows long; in some block it is exactly 512 rows long. `assignment`: every block index is named by exactly 1 sequence. Within a sequence, positions rise by one from row to row from a start between 0 and 2048 minus the sequence's length; empty rows hold 0.
All inputs are finite; a program needn't handle non-finite values.
Results may differ from a plain program's by a relative error of at most 0.023.
Values may be sent and summed in bfloat16 or wider, within the bound.
A program may use at most 192 MiB of HBM per device.

v0:
```python
import math
import jax
import jax.numpy as jnp
from jax import lax
from jax.sharding import PartitionSpec as P

HEADS = 12
HDIM = 64
EPSILON = 1e-05
ROPE_BASE = 10000.0


def rms_scale(values):
    return lax.rsqrt(jnp.mean(values * values, axis=-1, keepdims=True) + EPSILON)


def rotation(positions, head_size):
    half_size = head_size // 2
    steps_range = jnp.arange(half_size, dtype=jnp.float32)
    frequency = jnp.exp(steps_range * (-2.0 * math.log(ROPE_BASE) / head_size))
    angles = positions.astype(jnp.float32)[:, None] * frequency[None, :]
    return (jnp.cos(angles), jnp.sin(angles))


def rotate(values, cosine_table, sine_table):
    half_size = cosine_table.shape[1]
    shaped = values.reshape(values.shape[0], -1, 2 * half_size)
    first_half = shaped[..., :half_size]
    second_half = shaped[..., half_size:]
    cos_rows = cosine_table[:, None, :]
    sin_rows = sine_table[:, None, :]
    turned = jnp.concatenate(
        [
            first_half * cos_rows - second_half * sin_rows,
            second_half * cos_rows + first_half * sin_rows,
        ],
        axis=-1,
    )
    return turned.reshape(values.shape)


def rotate_back(values, cosine_table, sine_table):
    half_size = cosine_table.shape[1]
    shaped = values.reshape(values.shape[0], -1, 2 * half_size)
    first_half = shaped[..., :half_size]
    second_half = shaped[..., half_size:]
    cos_rows = cosine_table[:, None, :]
    sin_rows = sine_table[:, None, :]
    turned = jnp.concatenate(
        [
            first_half * cos_rows + second_half * sin_rows,
            second_half * cos_rows - first_half * sin_rows,
        ],
        axis=-1,
    )
    return turned.reshape(values.shape)


def sequence_mask(lengths, assignment, device, slot_count):
    owned_lengths = jnp.where(assignment == device, lengths, 0)
    seq_ends = jnp.cumsum(owned_lengths)
    slot_ids = jnp.arange(slot_count, dtype=jnp.int32)
    labels = jnp.sum((seq_ends[None, :] <= slot_ids[:, None]).astype(jnp.int32), axis=1)
    allowed = (labels[:, None] == labels[None, :]) & (slot_ids[None, :] <= slot_ids[:, None])
    valid_rows = (slot_ids < seq_ends[-1]).astype(jnp.float32)[:, None]
    return (allowed, valid_rows)


def by_group(values, groups):
    return jnp.moveaxis(values.reshape(values.shape[0], groups, -1, HDIM), 1, 0)


def from_group(values):
    moved = jnp.moveaxis(values, 0, 1)
    return moved.reshape(moved.shape[0], -1)


def norm_back(grad_normed, values, scale_rows, gain):
    scaled_grad = gain * grad_normed
    gain_grad = jnp.sum(grad_normed * values * scale_rows, axis=0)
    grad_values = scale_rows * scaled_grad - values * scale_rows**3 * jnp.mean(
        scaled_grad * values, axis=-1, keepdims=True
    )
    return (gain_grad, grad_values)


def per_device(
    tokens,
    cotangent,
    lengths,
    assignment,
    positions,
    attention_gain,
    query_weight,
    key_weight,
    value_weight,
    out_weight,
    feedforward_gain,
    gate_weight,
    up_weight,
    down_weight,
):
    slot_count = tokens.shape[0]
    heads_per = math.gcd(HEADS, 4)
    groups = HEADS // heads_per
    inv_root = 1.0 / math.sqrt(HDIM)
    device = lax.axis_index("shard") * lax.axis_size("replica") + lax.axis_index("replica")
    allowed, valid_rows = sequence_mask(lengths, assignment, device, slot_count)
    cosine_table, sine_table = rotation(positions, HDIM)
    gain_one, w_query, w_key, w_value, w_out = (
        lax.all_gather(attention_gain, "shard", axis=0, tiled=True),
        lax.all_gather(query_weight, "shard", axis=0, tiled=True),
        lax.all_gather(key_weight, "shard", axis=0, tiled=True),
        lax.all_gather(value_weight, "shard", axis=0, tiled=True),
        lax.all_gather(out_weight, "shard", axis=0, tiled=True),
    )
    values = tokens.astype(jnp.float32)
    scale_one = rms_scale(values)
    normed = (values * scale_one * gain_one.astype(jnp.float32)).astype(jnp.bfloat16)
    query_lin = jnp.dot(normed, w_query, preferred_element_type=jnp.float32)
    key_lin = jnp.dot(normed, w_key, preferred_element_type=jnp.float32)
    value_low = jnp.dot(normed, w_value, preferred_element_type=jnp.float32).astype(jnp.bfloat16)
    query_rot = rotate(query_lin, cosine_table, sine_table).astype(jnp.bfloat16)
    key_rot = rotate(key_lin, cosine_table, sine_table).astype(jnp.bfloat16)
    query_groups = by_group(query_rot, groups)
    key_groups = by_group(key_rot, groups)
    value_groups = by_group(value_low, groups)

    def attend(group_in):
        query_part, key_part, value_part = group_in
        scores = (
            jnp.einsum("qhd,khd->hqk", query_part, key_part, preferred_element_type=jnp.float32)
            * inv_root
        )
        scores = jnp.where(allowed[None], scores, -jnp.inf)
        row_peak = jnp.max(scores, axis=-1, keepdims=True)
        exponent = jnp.exp(scores - row_peak)
        row_total = jnp.sum(exponent, axis=-1, keepdims=True)
        probability = (exponent / row_total).astype(jnp.bfloat16)
        mixed_values = jnp.einsum(
            "hqk,khd->qhd", probability, value_part, preferred_element_type=jnp.float32
        )
        return (mixed_values, row_peak[..., 0] + jnp.log(row_total[..., 0]))

    mixed_groups, log_totals = lax.map(attend, (query_groups, key_groups, value_groups))
    attended = from_group(mixed_groups).astype(jnp.bfloat16)
    hidden_one = values + jnp.dot(attended, w_out, preferred_element_type=jnp.float32)
    gain_two, w_gate, w_up, w_down = (
        lax.all_gather(feedforward_gain, "shard", axis=0, tiled=True),
        lax.all_gather(gate_weight, "shard", axis=0, tiled=True),
        lax.all_gather(up_weight, "shard", axis=0, tiled=True),
        lax.all_gather(down_weight, "shard", axis=0, tiled=True),
    )
    scale_two = rms_scale(hidden_one)
    normed_two = (hidden_one * scale_two * gain_two.astype(jnp.float32)).astype(jnp.bfloat16)
    gate = jnp.dot(normed_two, w_gate, preferred_element_type=jnp.float32)
    upward = jnp.dot(normed_two, w_up, preferred_element_type=jnp.float32)
    sigmoid_gate = jax.nn.sigmoid(gate)
    activated = gate * sigmoid_gate
    hidden = (activated * upward).astype(jnp.bfloat16)
    branch_two = jnp.dot(hidden, w_down, preferred_element_type=jnp.float32)
    output = ((hidden_one + branch_two) * valid_rows).astype(jnp.bfloat16)
    gain_two, w_gate, w_up, w_down = (
        lax.all_gather(feedforward_gain, "shard", axis=0, tiled=True),
        lax.all_gather(gate_weight, "shard", axis=0, tiled=True),
        lax.all_gather(up_weight, "shard", axis=0, tiled=True),
        lax.all_gather(down_weight, "shard", axis=0, tiled=True),
    )
    grad_out = cotangent.astype(jnp.float32) * valid_rows
    grad_branch_two = grad_out.astype(jnp.bfloat16)
    grad_down = jnp.einsum("nf,nd->fd", hidden, grad_branch_two, preferred_element_type=jnp.float32)
    grad_hidden = jnp.einsum(
        "nd,fd->nf", grad_branch_two, w_down, preferred_element_type=jnp.float32
    )
    grad_gate = (grad_hidden * upward * sigmoid_gate * (1.0 + gate * (1.0 - sigmoid_gate))).astype(
        jnp.bfloat16
    )
    grad_up = (grad_hidden * activated).astype(jnp.bfloat16)
    grad_gate_weight = jnp.einsum(
        "nd,nf->df", normed_two, grad_gate, preferred_element_type=jnp.float32
    )
    grad_up_weight = jnp.einsum(
        "nd,nf->df", normed_two, grad_up, preferred_element_type=jnp.float32
    )
    grad_normed_two = jnp.einsum(
        "nf,df->nd", grad_gate, w_gate, preferred_element_type=jnp.float32
    ) + jnp.einsum("nf,df->nd", grad_up, w_up, preferred_element_type=jnp.float32)
    grad_gain_two, grad_norm_two = norm_back(
        grad_normed_two, hidden_one, scale_two, gain_two.astype(jnp.float32)
    )
    grad_hidden_one = grad_out + grad_norm_two
    ffn_terms = (grad_gain_two, grad_gate_weight, grad_up_weight, grad_down)
    ffn_shares = (
        lax.psum_scatter(
            ffn_terms[0].astype(jnp.bfloat16), "shard", scatter_dimension=0, tiled=True
        ).astype(jnp.float32),
        lax.psum_scatter(
            ffn_terms[1].astype(jnp.bfloat16), "shard", scatter_dimension=0, tiled=True
        ).astype(jnp.float32),
        lax.psum_scatter(
            ffn_terms[2].astype(jnp.bfloat16), "shard", scatter_dimension=0, tiled=True
        ).astype(jnp.float32),
        lax.psum_scatter(
            ffn_terms[3].astype(jnp.bfloat16), "shard", scatter_dimension=0, tiled=True
        ).astype(jnp.float32),
    )
    ffn_sums = (
        lax.psum(ffn_shares[0].astype(jnp.bfloat16), "replica").astype(jnp.float32),
        lax.psum(ffn_shares[1].astype(jnp.bfloat16), "replica").astype(jnp.float32),
        lax.psum(ffn_shares[2].astype(jnp.bfloat16), "replica").astype(jnp.float32),
        lax.psum(ffn_shares[3].astype(jnp.bfloat16), "replica").astype(jnp.float32),
    )
    gain_one, w_query, w_key, w_value, w_out = (
        lax.all_gather(attention_gain, "shard", axis=0, tiled=True),
        lax.all_gather(query_weight, "shard", axis=0, tiled=True),
        lax.all_gather(key_weight, "shard", axis=0, tiled=True),
        lax.all_gather(value_weight, "shard", axis=0, tiled=True),
        lax.all_gather(out_weight, "shard", axis=0, tiled=True),
    )
    grad_branch_one = grad_hidden_one.astype(jnp.bfloat16)
    grad_out_weight = jnp.einsum(
        "nd,ne->de", attended, grad_branch_one, preferred_element_type=jnp.float32
    )
    grad_attended = jnp.einsum(
        "ne,de->nd", grad_branch_one, w_out, preferred_element_type=jnp.float32
    ).astype(jnp.bfloat16)
    grad_groups = by_group(grad_attended, groups)

    def attend_back(group_in):
        query_part, key_part, value_part, grad_part, log_total = group_in
        scores = (
            jnp.einsum("qhd,khd->hqk", query_part, key_part, preferred_element_type=jnp.float32)
            * inv_root
        )
        scores = jnp.where(allowed[None], scores, -jnp.inf)
        probability = jnp.exp(scores - log_total[..., None])
        probability_low = probability.astype(jnp.bfloat16)
        grad_value = jnp.einsum(
            "hqk,qhd->khd", probability_low, grad_part, preferred_element_type=jnp.float32
        )
        grad_probability = jnp.einsum(
            "qhd,khd->hqk", grad_part, value_part, preferred_element_type=jnp.float32
        )
        row_dot = jnp.sum(probability * grad_probability, axis=-1, keepdims=True)
        grad_scores = (probability * (grad_probability - row_dot)).astype(jnp.bfloat16)
        grad_query = (
            jnp.einsum("hqk,khd->qhd", grad_scores, key_part, preferred_element_type=jnp.float32)
            * inv_root
        )
        grad_key = (
            jnp.einsum("hqk,qhd->khd", grad_scores, query_part, preferred_element_type=jnp.float32)
            * inv_root
        )
        return (grad_query, grad_key, grad_value)

    grad_query_groups, grad_key_groups, grad_value_groups = lax.map(
        attend_back, (query_groups, key_groups, value_groups, grad_groups, log_totals)
    )
    grad_query_lin = rotate_back(from_group(grad_query_groups), cosine_table, sine_table).astype(
        jnp.bfloat16
    )
    grad_key_lin = rotate_back(from_group(grad_key_groups), cosine_table, sine_table).astype(
        jnp.bfloat16
    )
    grad_value_lin = from_group(grad_value_groups).astype(jnp.bfloat16)
    grad_query_weight = jnp.einsum(
        "nd,ne->de", normed, grad_query_lin, preferred_element_type=jnp.float32
    )
    grad_key_weight = jnp.einsum(
        "nd,ne->de", normed, grad_key_lin, preferred_element_type=jnp.float32
    )
    grad_value_weight = jnp.einsum(
        "nd,ne->de", normed, grad_value_lin, preferred_element_type=jnp.float32
    )
    grad_normed = jnp.einsum(
        "ne,de->nd", grad_query_lin, w_query, preferred_element_type=jnp.float32
    )
    grad_normed = grad_normed + jnp.einsum(
        "ne,de->nd", grad_key_lin, w_key, preferred_element_type=jnp.float32
    )
    grad_normed = grad_normed + jnp.einsum(
        "ne,de->nd", grad_value_lin, w_value, preferred_element_type=jnp.float32
    )
    grad_gain_one, grad_norm_one = norm_back(
        grad_normed, values, scale_one, gain_one.astype(jnp.float32)
    )
    input_grad = grad_hidden_one + grad_norm_one
    attn_terms = (
        grad_gain_one,
        grad_query_weight,
        grad_key_weight,
        grad_value_weight,
        grad_out_weight,
    )
    attn_shares = (
        lax.psum_scatter(
            attn_terms[0].astype(jnp.bfloat16), "shard", scatter_dimension=0, tiled=True
        ).astype(jnp.float32),
        lax.psum_scatter(
            attn_terms[1].astype(jnp.bfloat16), "shard", scatter_dimension=0, tiled=True
        ).astype(jnp.float32),
        lax.psum_scatter(
            attn_terms[2].astype(jnp.bfloat16), "shard", scatter_dimension=0, tiled=True
        ).astype(jnp.float32),
        lax.psum_scatter(
            attn_terms[3].astype(jnp.bfloat16), "shard", scatter_dimension=0, tiled=True
        ).astype(jnp.float32),
        lax.psum_scatter(
            attn_terms[4].astype(jnp.bfloat16), "shard", scatter_dimension=0, tiled=True
        ).astype(jnp.float32),
    )
    attn_sums = (
        lax.psum(attn_shares[0].astype(jnp.bfloat16), "replica").astype(jnp.float32),
        lax.psum(attn_shares[1].astype(jnp.bfloat16), "replica").astype(jnp.float32),
        lax.psum(attn_shares[2].astype(jnp.bfloat16), "replica").astype(jnp.float32),
        lax.psum(attn_shares[3].astype(jnp.bfloat16), "replica").astype(jnp.float32),
        lax.psum(attn_shares[4].astype(jnp.bfloat16), "replica").astype(jnp.float32),
    )
    return (
        output,
        input_grad,
        attn_sums[0],
        attn_sums[1],
        attn_sums[2],
        attn_sums[3],
        attn_sums[4],
        ffn_sums[0],
        ffn_sums[1],
        ffn_sums[2],
        ffn_sums[3],
    )


def solution(mesh):
    return jax.shard_map(
        per_device,
        mesh=mesh,
        in_specs=(
            P(("shard", "replica"), None),
            P(("shard", "replica"), None),
            P(),
            P(),
            P(("shard", "replica")),
            P("shard"),
            P("shard", None),
            P("shard", None),
            P("shard", None),
            P("shard", None),
            P("shard"),
            P("shard", None),
            P("shard", None),
            P("shard", None),
        ),
        out_specs=(
            P(("shard", "replica"), None),
            P(("shard", "replica"), None),
            P("shard"),
            P("shard", None),
            P("shard", None),
            P("shard", None),
            P("shard", None),
            P("shard"),
            P("shard", None),
            P("shard", None),
            P("shard", None),
        ),
        check_vma=False,
    )
```

profile of v0, /device:TPU:0, one launch (start us, length us, event | category | flops | bytes accessed | tf_op | source)
XLA Modules:
  0.0 718.3 jit_solution(7855634631792464619)
XLA Ops:
  15.5 8.7 %all-reduce.7 = (bf16[768]{0:T(1024)(128)(2,1)S(1)}, bf16[768]{0:T(1024)(128)(2,1)S(1)}) all-reduce(bf16[768]{0:T(1024)(128)(2,1)S(1)} %dynamic-update-slice, bf16[768]{0:T(1024)(128)(2,1)S(1)} %dynamic-update-slice.1), channel_id=1, replica_groups=mesh['shard'=4,'replica'=8] {'shard'}, use_global_device_ids=true, to_apply=%add | all-reduce | flops 1536 | bytes 6144
  33.0 15.8 %all-gather.10.cloned.1.call-done = bf16[768,768]{1,0:T(8,128)(2,1)} async-done(((bf16[192,768]{1,0:T(8,128)(2,1)}), bf16[768,768]{1,0:T(8,128)(2,1)}) %all-gather.10.cloned.1.call-update) | async-done | bytes 1179664 | tf_op jit(solution)/shard_map/all_gather | solution.py:112
  51.1 16.9 %all-gather.12.cloned.1.call-done = bf16[768,768]{1,0:T(8,128)(2,1)} async-done(((bf16[192,768]{1,0:T(8,128)(2,1)}), bf16[768,768]{1,0:T(8,128)(2,1)}) %all-gather.12.cloned.1.call-update) | async-done | bytes 1179664 | tf_op jit(solution)/shard_map/all_gather | solution.py:113
  70.8 15.3 %while.30 = (s32[]{:T(128)}, bf16[3,512,4,64]{1,3,2,0:T(8,128)(2,1)}, f32[3,4,512]{2,1,0:T(4,128)S(1)}, bf16[3,512,4,64]{1,3,2,0:T(8,128)(2,1)}, bf16[3,512,4,64...) while((s32[]{:T(128)}, ...), condition=%wide.region_6.7_spmd.clone.clone, body=%wide.region_3.6_spmd.clone.sunk.clone | while | flops 281802752 | bytes 15011921 | solution.py:145
  72.8 3.0 fusion.166
  77.9 3.0 fusion.166
  83.0 3.0 fusion.166
  90.6 35.1 %all-gather.16.cloned.1.call-done = bf16[768,3072]{1,0:T(8,128)(2,1)} async-done(((bf16[192,3072]{1,0:T(8,128)(2,1)}), bf16[768,3072]{1,0:T(8,128)(2,1)}) %all-gather.16.cloned.1.call-update) | async-done | bytes 4718608 | tf_op jit(solution)/shard_map/all_gather | solution.py:150
  125.7 6.8 fusion.87
  132.5 32.1 %all-gather.18.cloned.1.call-done = bf16[768,3072]{1,0:T(8,128)(2,1)} async-done(((bf16[192,3072]{1,0:T(8,128)(2,1)}), bf16[768,3072]{1,0:T(8,128)(2,1)}) %all-gather.18.cloned.1.call-update) | async-done | bytes 4718608 | tf_op jit(solution)/shard_map/all_gather | solution.py:151
  164.6 6.8 fusion.88
  171.4 32.2 %all-gather.20.cloned.1.call-done = bf16[3072,768]{1,0:T(8,128)(2,1)} async-done(((bf16[768,768]{1,0:T(8,128)(2,1)}), bf16[3072,768]{1,0:T(8,128)(2,1)}) %all-gather.20.cloned.1.call-update) | async-done | bytes 4718608 | tf_op jit(solution)/shard_map/all_gather | solution.py:152
  203.6 10.4 %multiply_convert_fusion.1 = (bf16[512,3072]{1,0:T(8,128)(2,1)S(1)}, bf16[512,3072]{1,0:T(8,128)(2,1)S(1)}, bf16[512,3072]{1,0:T(8,128)(2,1)}) fusion(f32[512,3072]{1,0:T(8,128)} %fusion.87, f32[512,3072]{1,0:T(8,128)} %fusion.88, bf16[3072,768]{1,0:T(8,128)(2,1)} %all-gather.20.cloned.1.call-done, bf16[512,768]{1,0:T(8,128)(2,1)S(1)} %copy-done.12, ...), kind=kOutput, calls=%fused_computation.64 | convolution fusion | flops 2440691712 | bytes 27527168 | tf_op jit(solution)/shard_map/nd,fd->nf/dot_general | solution.py:172
  214.0 7.3 %fusion.89 = f32[512,768]{1,0:T(8,128)S(1)} fusion(bf16[512,3072]{1,0:T(8,128)(2,1)S(1)} %get-tuple-element.204, bf16[768,3072]{1,0:T(8,128)(2,1)} %all-gather.16.cloned.1.call-done), kind=kOutput, calls=%fused_computation.139 | convolution fusion | flops 2415919104 | bytes 9437184 | tf_op jit(solution)/shard_map/nf,df->nd/dot_general | solution.py:185
  229.7 28.9 %while.31 = (s32[]{:T(128)}, f32[3,512,4,64]{1,3,2,0:T(8,128)}, f32[3,512,4,64]{1,3,2,0:T(8,128)}, bf16[3,512,4,64]{1,3,2,0:T(8,128)(2,1)}, bf16[3,512,4,64]{1,3...) while((s32[]{:T(128)}, f32[3,512,4,64]{1,3,2,0:T(8,128)}, ...), condition=%wide.region_11.12_spmd.clone.clone, body=%wide.region_9.11_spmd.clone.sunk.clone | while | flops 687863808 | bytes 39124100 | solution.py:256
  270.5 3.3 convolution_convert_fusion.4
  273.8 6.2 convolution_convert_fusion.2
  280.1 6.3 convolution_convert_fusion.1
  287.6 6.8 convolution_convert_fusion
  294.5 24.4 %reduce-scatter.8.cloned.1.call-done = bf16[192,768]{1,0:T(8,128)(2,1)} async-done(((bf16[768,768]{1,0:T(8,128)(2,1)}), bf16[192,768]{1,0:T(8,128)(2,1)}) %reduce-scatter.8.cloned.1.call-update) | async-done | bytes 294928 | tf_op jit(solution)/shard_map/reduce_scatter | solution.py:299
  319.0 28.1 %reduce-scatter.14.cloned.1.call-done = bf16[192,768]{1,0:T(8,128)(2,1)} async-done(((bf16[768,768]{1,0:T(8,128)(2,1)}), bf16[192,768]{1,0:T(8,128)(2,1)}) %reduce-scatter.14.cloned.1.call-update) | async-done | bytes 294928 | tf_op jit(solution)/shard_map/reduce_scatter | solution.py:308
  347.0 28.8 %reduce-scatter.12.cloned.1.call-done = bf16[192,768]{1,0:T(8,128)(2,1)} async-done(((bf16[768,768]{1,0:T(8,128)(2,1)}), bf16[192,768]{1,0:T(8,128)(2,1)}) %reduce-scatter.12.cloned.1.call-update) | async-done | bytes 294928 | tf_op jit(solution)/shard_map/reduce_scatter | solution.py:305
  375.8 50.4 %reduce-scatter.16.cloned.1.call-done = bf16[192,3072]{1,0:T(8,128)(2,1)} async-done(((bf16[768,3072]{1,0:T(8,128)(2,1)}), bf16[192,3072]{1,0:T(8,128)(2,1)}) %reduce-scatter.16.cloned.1.call-update) | async-done | bytes 1179664 | tf_op jit(solution)/shard_map/reduce_scatter | solution.py:197
  426.2 50.5 %reduce-scatter.18.cloned.1.call-done = bf16[192,3072]{1,0:T(8,128)(2,1)} async-done(((bf16[768,3072]{1,0:T(8,128)(2,1)}), bf16[192,3072]{1,0:T(8,128)(2,1)}) %reduce-scatter.18.cloned.1.call-update) | async-done | bytes 1179664 | tf_op jit(solution)/shard_map/reduce_scatter | solution.py:200
  476.7 50.4 %reduce-scatter.20.cloned.1.call-done = bf16[768,768]{1,0:T(8,128)(2,1)} async-done(((bf16[3072,768]{1,0:T(8,128)(2,1)}), bf16[768,768]{1,0:T(8,128)(2,1)}) %reduce-scatter.20.cloned.1.call-update) | async-done | bytes 1179664 | tf_op jit(solution)/shard_map/reduce_scatter | solution.py:203
  531.8 3.5 fusion.68
  535.2 5.7 all-reduce.6
  541.1 23.0 %all-reduce.4 = (bf16[192]{0:T(256)(128)(2,1)S(1)}, bf16[192]{0:T(256)(128)(2,1)S(1)}) all-reduce(bf16[192]{0:T(256)(128)(2,1)S(1)} %dynamic-slice.3, bf16[192]{0:T(256)(128)(2,1)S(1)} %dynamic-slice.5), channel_id=1, replica_groups=mesh['shard'=4,'replica'=8] {'replica'}, use_global_device_ids=true, to_apply=%region_15.16 | all-reduce | flops 384 | bytes 1536 | tf_op jit(solution)/shard_map/psum | solution.py:313
  565.2 3.1 fusion.65
  568.4 5.8 multiply_convert_fusion.4
  574.2 127.6 %all-reduce.10.cloned.1.call-done = (bf16[192,768]{1,0:T(8,128)(2,1)}, bf16[192,768]{1,0:T(8,128)(2,1)}, bf16[192,768]{1,0:T(8,128)(2,1)}, bf16[192,768]{1,0:T(8...) async-done(((bf16[192,768]{1,0:T(8,128)(2,1)}, bf16[192,768]{1,0:T(8,128)(2,1)}, bf16[192,768]{1,0:T(8,128)(2,1)}, ...) | async-done | bytes 4718608 | tf_op jit(solution)/shard_map/psum | solution.py:314
  701.8 3.0 convert_element_type.214
  (200 shorter events, 93.9 us)
Async XLA Ops:
  7.2 22.6 %all-gather.8.cloned.1.call-start = ((), (), s32[]{:S(2)}) async-start(), calls=%async_computation.7 | async-start | bytes 1474560 | tf_op jit(solution)/shard_map/all_gather | solution.py:114
  7.9 41.0 %all-gather.10.cloned.1.call-start = ((), (), s32[]{:S(2)}) async-start(), calls=%async_computation.8 | async-start | bytes 1474560 | tf_op jit(solution)/shard_map/all_gather | solution.py:112
  8.7 59.3 %all-gather.12.cloned.1.call-start = ((), (), s32[]{:S(2)}) async-start(), calls=%async_computation.9 | async-start | bytes 1474560 | tf_op jit(solution)/shard_map/all_gather | solution.py:113
  9.4 77.4 %all-gather.14.cloned.1.call-start = ((), (), s32[]{:S(2)}) async-start(), calls=%async_computation.10 | async-start | bytes 1474560 | tf_op jit(solution)/shard_map/all_gather | solution.py:115
  10.0 115.7 %all-gather.16.cloned.1.call-start = ((), (), s32[]{:S(2)}) async-start(), calls=%async_computation.11 | async-start | bytes 5898240 | tf_op jit(solution)/shard_map/all_gather | solution.py:150
  10.6 3.2 copy-start.24
  10.6 4.4 copy-start.30
  10.6 4.7 copy-start.31
  10.6 13.6 %copy-start = (bf16[512,768]{1,0:T(8,128)(2,1)S(1)}, bf16[512,768]{1,0:T(8,128)(2,1)}, u32[]{:S(2)}) copy-start(bf16[512,768]{1,0:T(8,128)(2,1)} %param.18) | copy-start | bytes 2359300
  10.6 153.9 %all-gather.18.cloned.1.call-start = ((), (), s32[]{:S(2)}) async-start(), calls=%async_computation.12 | async-start | bytes 5898240 | tf_op jit(solution)/shard_map/all_gather | solution.py:151
  11.2 13.8 %copy-start.25 = (s32[512]{0:T(512)S(1)}, s32[512]{0:T(512)}, u32[]{:S(2)}) copy-start(s32[512]{0:T(512)} %param.22) | copy-start | bytes 6148
  11.2 192.4 %all-gather.20.cloned.1.call-start = ((), (), s32[]{:S(2)}) async-start(), calls=%async_computation.13 | async-start | bytes 5898240 | tf_op jit(solution)/shard_map/all_gather | solution.py:152
  12.0 282.6 %reduce-scatter.10.cloned.1.call-start = ((), (), s32[]{:S(2)}) async-start(), calls=%async_computation.15 | async-start | bytes 1474560 | tf_op jit(solution)/shard_map/reduce_scatter | solution.py:302
  90.6 74.0 %copy-start.2 = (bf16[512,768]{1,0:T(8,128)(2,1)}, bf16[512,768]{1,0:T(8,128)(2,1)S(1)}, u32[]{:S(2)}) copy-start(bf16[512,768]{1,0:T(8,128)(2,1)S(1)} %multiply_convert_fusion.5) | copy-start | bytes 2359300
  132.5 71.1 %copy-start.12 = (bf16[512,768]{1,0:T(8,128)(2,1)S(1)}, bf16[512,768]{1,0:T(8,128)(2,1)}, u32[]{:S(2)}) copy-start(bf16[512,768]{1,0:T(8,128)(2,1)} %param.19) | copy-start | bytes 2359300
  214.0 7.3 %copy-start.33 = (bf16[512,3072]{1,0:T(8,128)(2,1)}, bf16[512,3072]{1,0:T(8,128)(2,1)S(1)}, u32[]{:S(2)}) copy-start(bf16[512,3072]{1,0:T(8,128)(2,1)S(1)} %get-tuple-element.204) | copy-start | bytes 9437188
  214.0 7.3 %copy-start.32 = (bf16[512,3072]{1,0:T(8,128)(2,1)}, bf16[512,3072]{1,0:T(8,128)(2,1)S(1)}, u32[]{:S(2)}) copy-start(bf16[512,3072]{1,0:T(8,128)(2,1)S(1)} %get-tuple-element.203) | copy-start | bytes 9437188
  214.0 7.3 %copy-start.5 = (f32[512,768]{1,0:T(8,128)S(1)}, f32[512,768]{1,0:T(8,128)}, u32[]{:S(2)}) copy-start(f32[512,768]{1,0:T(8,128)} %copy-done.4) | copy-start | bytes 4718596
  214.0 7.3 %copy-start.8 = (bf16[768,3072]{1,0:T(8,128)(2,1)S(1)}, bf16[768,3072]{1,0:T(8,128)(2,1)}, u32[]{:S(2)}) copy-start(bf16[768,3072]{1,0:T(8,128)(2,1)} %all-gather.18.cloned.1.call-done) | copy-start | bytes 14155780
  221.3 3.0 copy-start.13
  264.4 54.6 %reduce-scatter.8.cloned.1.call-start = ((), (), s32[]{:S(2)}) async-start(), calls=%async_computation.14 | async-start | bytes 1474560 | tf_op jit(solution)/shard_map/reduce_scatter | solution.py:299
  267.4 79.6 %reduce-scatter.14.cloned.1.call-start = ((), (), s32[]{:S(2)}) async-start(), calls=%async_computation.17 | async-start | bytes 1474560 | tf_op jit(solution)/shard_map/reduce_scatter | solution.py:308
  270.4 105.4 %reduce-scatter.12.cloned.1.call-start = ((), (), s32[]{:S(2)}) async-start(), calls=%async_computation.16 | async-start | bytes 1474560 | tf_op jit(solution)/shard_map/reduce_scatter | solution.py:305
  270.5 3.3 copy-start.3
  273.8 152.4 %reduce-scatter.16.cloned.1.call-start = ((), (), s32[]{:S(2)}) async-start(), calls=%async_computation.18 | async-start | bytes 5898240 | tf_op jit(solution)/shard_map/reduce_scatter | solution.py:197
  280.1 196.6 %reduce-scatter.18.cloned.1.call-start = ((), (), s32[]{:S(2)}) async-start(), calls=%async_computation.19 | async-start | bytes 5898240 | tf_op jit(solution)/shard_map/reduce_scatter | solution.py:200
  286.5 240.6 %reduce-scatter.20.cloned.1.call-start = ((), (), s32[]{:S(2)}) async-start(), calls=%async_computation.20 | async-start | bytes 5898240 | tf_op jit(solution)/shard_map/reduce_scatter | solution.py:203
  294.4 407.3 %all-reduce.10.cloned.1.call-start = ((), (), s32[]{:S(2)}) async-start(), calls=%async_computation.21 | async-start | bytes 9437184 | tf_op jit(solution)/shard_map/psum | solution.py:314
  531.8 33.5 %copy-start.23 = (f32[512]{0:T(512)S(1)}, f32[512]{0:T(512)}, u32[]{:S(2)}) copy-start(f32[512]{0:T(512)} %get-tuple-element.222) | copy-start | bytes 6148
  565.2 3.1 copy-start.6
  565.2 3.1 copy-start.34
  701.8 3.0 copy-start.11
  (20 other events, 31.9 us)
Sparse Core Ops, SparseCore 0:
  9.5 20.1 all-gather.7
  31.3 17.5 all-gather.9
  50.4 17.4 all-gather.11
  69.3 17.4 all-gather.13
  88.2 37.4 all-gather.15
  127.1 37.4 all-gather.17
  166.1 37.4 all-gather.19
  264.5 25.6 reduce-scatter.9
  293.3 25.6 reduce-scatter.7
  321.4 25.6 reduce-scatter.13
  350.2 25.6 reduce-scatter.11
  378.2 47.9 reduce-scatter.15
  428.7 47.9 reduce-scatter.17
  479.1 47.9 reduce-scatter.19
  531.5 170.2 all-reduce.9
where the time goes:
time: 728 us; the launch traced here: 718 us
  waiting for transfers between devices  499 us (69%)
  matrix products  122 us (17%)
  blocking collectives  37.4 us (5%)
  other arithmetic  28.5 us (4%)
  between operations  15.9 us (2%)
  local copies, waits for them, and re-layouts  13.8 us (2%)
    psum x1, waiting for transfers between devices, per_device(): lax.psum(attn_shares[1].astype(jnp.bfloat16), 'replica').astype(jnp.float32)  128 us
    reduce_scatter x1, waiting for transfers between devices, per_device(): lax.psum_scatter(ffn_terms[2].astype(jnp.bfloat16), 'shard', scatter_dime...  50.5 us
    reduce_scatter x1, waiting for transfers between devices, per_device(): lax.psum_scatter(ffn_terms[1].astype(jnp.bfloat16), 'shard', scatter_dime...  50.4 us
    reduce_scatter x1, waiting for transfers between devices, per_device(): lax.psum_scatter(ffn_terms[3].astype(jnp.bfloat16), 'shard', scatter_dime...  50.4 us
    all_gather x1, waiting for transfers between devices, per_device(): lax.all_gather(gate_weight, 'shard', axis=0, tiled=True)  35.1 us
    all_gather x1, waiting for transfers between devices, per_device(): lax.all_gather(down_weight, 'shard', axis=0, tiled=True)  32.2 us
    all_gather x1, waiting for transfers between devices, per_device(): lax.all_gather(up_weight, 'shard', axis=0, tiled=True)  32.1 us
    reduce_scatter x1, waiting for transfers between devices, per_device(): lax.psum_scatter(attn_terms[3].astype(jnp.bfloat16), 'shard', scatter_dim...  28.8 us
  transfers between devices with their start and end apart: 15, of which 14 were waited for; matrix products, arithmetic and copies ran while one was open for 13% of the time, Pallas kernels for 0%

commit v1 on v0

--- a/solution.py
+++ b/solution.py
@@ -311,7 +311,9 @@
     )
     attn_sums = (
         lax.psum(attn_shares[0].astype(jnp.bfloat16), "replica").astype(jnp.float32),
-        lax.psum(attn_shares[1].astype(jnp.bfloat16), "replica").astype(jnp.float32),
+        jnp.sum(lax.all_gather(attn_shares[1].astype(jnp.bfloat16), "replica"), axis=0).astype(
+            jnp.float32
+        ),
         lax.psum(attn_shares[2].astype(jnp.bfloat16), "replica").astype(jnp.float32),
         lax.psum(attn_shares[3].astype(jnp.bfloat16), "replica").astype(jnp.float32),
         lax.psum(attn_shares[4].astype(jnp.bfloat16), "replica").astype(jnp.float32),

time: 728 us -> 771 us (1.059)
  waiting for transfers between devices: 499 us -> 542 us
    psum x1, waiting for transfers between devices: 128 us -> 162 us  [per_device(): lax.psum(attn_shares[2].astype(jnp.bfloat16), 'replica').astype(jnp.float32)]
    reduce_scatter x1, waiting for transfers between devices: 24.4 us -> 0.02 us  [per_device(): lax.psum_scatter(attn_terms[1].astype(jnp.bfloat16), 'shard', scatter_dim...]
    reduce_scatter x1, waiting for transfers between devices: 0.02 us -> 23.9 us  [per_device(): lax.psum_scatter(attn_terms[2].astype(jnp.bfloat16), 'shard', scatter_dim...]
    all_gather x0 -> x1, waiting for transfers between devices: none -> 8.03 us  [per_device(): lax.all_gather(attn_shares[1].astype(jnp.bfloat16), 'replica')]
  transfers between devices with their start and end apart: 15 -> 16, of which waited for: 14 -> 15; matrix products, arithmetic and copies ran while one was open for 13% -> 12% of each run, Pallas kernels for 0% -> 0%
where the time goes in v1:
time: 771 us; the launch traced here: 762 us
  waiting for transfers between devices  542 us (70%)
  matrix products  122 us (16%)
  blocking collectives  36.2 us (5%)
  other arithmetic  30.6 us (4%)
  between operations  16 us (2%)
  local copies, waits for them, and re-layouts  13.8 us (2%)
    psum x1, waiting for transfers between devices, per_device(): lax.psum(attn_shares[2].astype(jnp.bfloat16), 'replica').astype(jnp.float32)  162 us
    reduce_scatter x1, waiting for transfers between devices, per_device(): lax.psum_scatter(ffn_terms[2].astype(jnp.bfloat16), 'shard', scatter_dime...  50.5 us
    reduce_scatter x1, waiting for transfers between devices, per_device(): lax.psum_scatter(ffn_terms[1].astype(jnp.bfloat16), 'shard', scatter_dime...  50.4 us
    reduce_scatter x1, waiting for transfers between devices, per_device(): lax.psum_scatter(ffn_terms[3].astype(jnp.bfloat16), 'shard', scatter_dime...  50.4 us
    all_gather x1, waiting for transfers between devices, per_device(): lax.all_gather(gate_weight, 'shard', axis=0, tiled=True)  35.1 us
    all_gather x1, waiting for transfers between devices, per_device(): lax.all_gather(down_weight, 'shard', axis=0, tiled=True)  32.2 us
    all_gather x1, waiting for transfers between devices, per_device(): lax.all_gather(up_weight, 'shard', axis=0, tiled=True)  32.1 us
    reduce_scatter x1, waiting for transfers between devices, per_device(): lax.psum_scatter(attn_terms[3].astype(jnp.bfloat16), 'shard', scatter_dim...  28.8 us
  transfers between devices with their start and end apart: 16, of which 15 were waited for; matrix products, arithmetic and copies ran while one was open for 12% of the time, Pallas kernels for 0%

profile of v1, /device:TPU:0, one launch (start us, length us, event | category | flops | bytes accessed | tf_op | source)
XLA Modules:
  0.0 761.8 jit_solution(1210851081440912295)
XLA Ops:
  15.5 8.7 %all-reduce.7 = (bf16[768]{0:T(1024)(128)(2,1)S(1)}, bf16[768]{0:T(1024)(128)(2,1)S(1)}) all-reduce(bf16[768]{0:T(1024)(128)(2,1)S(1)} %dynamic-update-slice, bf16[768]{0:T(1024)(128)(2,1)S(1)} %dynamic-update-slice.1), channel_id=1, replica_groups=mesh['shard'=4,'replica'=8] {'shard'}, use_global_device_ids=true, to_apply=%add | all-reduce | flops 1536 | bytes 6144
  33.0 15.8 %all-gather.12.cloned.1.call-done = bf16[768,768]{1,0:T(8,128)(2,1)} async-done(((bf16[192,768]{1,0:T(8,128)(2,1)}), bf16[768,768]{1,0:T(8,128)(2,1)}) %all-gather.12.cloned.1.call-update) | async-done | bytes 1179664 | tf_op jit(solution)/shard_map/all_gather | solution.py:112
  51.1 16.9 %all-gather.14.cloned.1.call-done = bf16[768,768]{1,0:T(8,128)(2,1)} async-done(((bf16[192,768]{1,0:T(8,128)(2,1)}), bf16[768,768]{1,0:T(8,128)(2,1)}) %all-gather.14.cloned.1.call-update) | async-done | bytes 1179664 | tf_op jit(solution)/shard_map/all_gather | solution.py:113
  70.8 15.3 %while.30 = (s32[]{:T(128)}, bf16[3,512,4,64]{1,3,2,0:T(8,128)(2,1)}, f32[3,4,512]{2,1,0:T(4,128)S(1)}, bf16[3,512,4,64]{1,3,2,0:T(8,128)(2,1)}, bf16[3,512,4,64...) while((s32[]{:T(128)}, ...), condition=%wide.region_6.7_spmd.clone.clone, body=%wide.region_3.6_spmd.clone.sunk.clone | while | flops 281802752 | bytes 15011921 | solution.py:145
  72.8 3.0 fusion.166
  77.9 3.0 fusion.166
  83.0 3.0 fusion.166
  90.6 35.1 %all-gather.18.cloned.1.call-done = bf16[768,3072]{1,0:T(8,128)(2,1)} async-done(((bf16[192,3072]{1,0:T(8,128)(2,1)}), bf16[768,3072]{1,0:T(8,128)(2,1)}) %all-gather.18.cloned.1.call-update) | async-done | bytes 4718608 | tf_op jit(solution)/shard_map/all_gather | solution.py:150
  125.7 6.8 fusion.87
  132.5 32.1 %all-gather.20.cloned.1.call-done = bf16[768,3072]{1,0:T(8,128)(2,1)} async-done(((bf16[192,3072]{1,0:T(8,128)(2,1)}), bf16[768,3072]{1,0:T(8,128)(2,1)}) %all-gather.20.cloned.1.call-update) | async-done | bytes 4718608 | tf_op jit(solution)/shard_map/all_gather | solution.py:151
  164.6 6.8 fusion.88
  171.4 32.2 %all-gather.22.cloned.1.call-done = bf16[3072,768]{1,0:T(8,128)(2,1)} async-done(((bf16[768,768]{1,0:T(8,128)(2,1)}), bf16[3072,768]{1,0:T(8,128)(2,1)}) %all-gather.22.cloned.1.call-update) | async-done | bytes 4718608 | tf_op jit(solution)/shard_map/all_gather | solution.py:152
  203.6 10.4 %multiply_convert_fusion.1 = (bf16[512,3072]{1,0:T(8,128)(2,1)S(1)}, bf16[512,3072]{1,0:T(8,128)(2,1)S(1)}, bf16[512,3072]{1,0:T(8,128)(2,1)}) fusion(f32[512,3072]{1,0:T(8,128)} %fusion.87, f32[512,3072]{1,0:T(8,128)} %fusion.88, bf16[3072,768]{1,0:T(8,128)(2,1)} %all-gather.22.cloned.1.call-done, bf16[512,768]{1,0:T(8,128)(2,1)S(1)} %copy-done.12, ...), kind=kOutput, calls=%fused_computation.64 | convolution fusion | flops 2440691712 | bytes 27527168 | tf_op jit(solution)/shard_map/nd,fd->nf/dot_general | solution.py:172
  214.0 7.3 fusion.89
  229.7 28.9 %while.31 = (s32[]{:T(128)}, f32[3,512,4,64]{1,3,2,0:T(8,128)}, f32[3,512,4,64]{1,3,2,0:T(8,128)}, bf16[3,512,4,64]{1,3,2,0:T(8,128)(2,1)}, bf16[3,512,4,64]{1,3...) while((s32[]{:T(128)}, f32[3,512,4,64]{1,3,2,0:T(8,128)}, ...), condition=%wide.region_11.12_spmd.clone.clone, body=%wide.region_9.11_spmd.clone.sunk.clone | while | flops 687863808 | bytes 39124100 | solution.py:256
  270.5 3.3 convolution_convert_fusion.4
  273.8 6.2 convolution_convert_fusion.2
  280.1 6.3 convolution_convert_fusion.1
  287.6 6.8 convolution_convert_fusion
  295.1 23.9 %reduce-scatter.10.cloned.1.call-done = bf16[192,768]{1,0:T(8,128)(2,1)} async-done(((bf16[768,768]{1,0:T(8,128)(2,1)}), bf16[192,768]{1,0:T(8,128)(2,1)}) %reduce-scatter.10.cloned.1.call-update) | async-done | bytes 294928 | tf_op jit(solution)/shard_map/reduce_scatter | solution.py:302
  319.0 28.1 %reduce-scatter.14.cloned.1.call-done = bf16[192,768]{1,0:T(8,128)(2,1)} async-done(((bf16[768,768]{1,0:T(8,128)(2,1)}), bf16[192,768]{1,0:T(8,128)(2,1)}) %reduce-scatter.14.cloned.1.call-update) | async-done | bytes 294928 | tf_op jit(solution)/shard_map/reduce_scatter | solution.py:308
  347.0 28.8 %reduce-scatter.12.cloned.1.call-done = bf16[192,768]{1,0:T(8,128)(2,1)} async-done(((bf16[768,768]{1,0:T(8,128)(2,1)}), bf16[192,768]{1,0:T(8,128)(2,1)}) %reduce-scatter.12.cloned.1.call-update) | async-done | bytes 294928 | tf_op jit(solution)/shard_map/reduce_scatter | solution.py:305
  375.8 50.4 %reduce-scatter.16.cloned.1.call-done = bf16[192,3072]{1,0:T(8,128)(2,1)} async-done(((bf16[768,3072]{1,0:T(8,128)(2,1)}), bf16[192,3072]{1,0:T(8,128)(2,1)}) %reduce-scatter.16.cloned.1.call-update) | async-done | bytes 1179664 | tf_op jit(solution)/shard_map/reduce_scatter | solution.py:197
  426.2 50.5 %reduce-scatter.18.cloned.1.call-done = bf16[192,3072]{1,0:T(8,128)(2,1)} async-done(((bf16[768,3072]{1,0:T(8,128)(2,1)}), bf16[192,3072]{1,0:T(8,128)(2,1)}) %reduce-scatter.18.cloned.1.call-update) | async-done | bytes 1179664 | tf_op jit(solution)/shard_map/reduce_scatter | solution.py:200
  476.8 50.4 %reduce-scatter.20.cloned.1.call-done = bf16[768,768]{1,0:T(8,128)(2,1)} async-done(((bf16[3072,768]{1,0:T(8,128)(2,1)}), bf16[768,768]{1,0:T(8,128)(2,1)}) %reduce-scatter.20.cloned.1.call-update) | async-done | bytes 1179664 | tf_op jit(solution)/shard_map/reduce_scatter | solution.py:203
  531.8 3.5 fusion.68
  535.3 5.7 all-reduce.6
  541.2 21.8 %all-reduce.4 = (bf16[192]{0:T(256)(128)(2,1)S(1)}, bf16[192]{0:T(256)(128)(2,1)S(1)}) all-reduce(bf16[192]{0:T(256)(128)(2,1)S(1)} %dynamic-slice.3, bf16[192]{0:T(256)(128)(2,1)S(1)} %dynamic-slice.5), channel_id=1, replica_groups=mesh['shard'=4,'replica'=8] {'replica'}, use_global_device_ids=true, to_apply=%region_15.16 | all-reduce | flops 384 | bytes 1536 | tf_op jit(solution)/shard_map/psum | solution.py:313
  564.1 3.1 fusion.65
  567.2 5.9 multiply_convert_fusion.4
  573.1 8.0 %all-gather.24.cloned.1.call-done = bf16[1536,768]{1,0:T(8,128)(2,1)} async-done(((bf16[192,768]{1,0:T(8,128)(2,1)}), bf16[1536,768]{1,0:T(8,128)(2,1)}) %all-gather.24.cloned.1.call-update) | async-done | bytes 2359312 | tf_op jit(solution)/shard_map/all_gather | solution.py:314
  584.1 162.2 %all-reduce.10.cloned.1.call-done = (bf16[192,768]{1,0:T(8,128)(2,1)}, bf16[192,768]{1,0:T(8,128)(2,1)}, bf16[192,768]{1,0:T(8,128)(2,1)}, bf16[192,3072]{1,0:T(...) async-done(((bf16[192,768]{1,0:T(8,128)(2,1)}, bf16[192,768]{1,0:T(8,128)(2,1)}, bf16[192,768]{1,0:T(8,128)(2,1)}, bf16[192,3072]{1,0:T(8,128)(2,1)}, ...) | async-done | bytes 4423696 | tf_op jit(solution)/shard_map/psum | solution.py:317
  (202 shorter events, 99.6 us)
Async XLA Ops:
  7.2 22.6 %all-gather.10.cloned.1.call-start = ((), (), s32[]{:S(2)}) async-start(), calls=%async_computation.7 | async-start | bytes 1474560 | tf_op jit(solution)/shard_map/all_gather | solution.py:114
  7.9 41.0 %all-gather.12.cloned.1.call-start = ((), (), s32[]{:S(2)}) async-start(), calls=%async_computation.8 | async-start | bytes 1474560 | tf_op jit(solution)/shard_map/all_gather | solution.py:112
  8.7 59.3 %all-gather.14.cloned.1.call-start = ((), (), s32[]{:S(2)}) async-start(), calls=%async_computation.9 | async-start | bytes 1474560 | tf_op jit(solution)/shard_map/all_gather | solution.py:113
  9.4 77.4 %all-gather.16.cloned.1.call-start = ((), (), s32[]{:S(2)}) async-start(), calls=%async_computation.10 | async-start | bytes 1474560 | tf_op jit(solution)/shard_map/all_gather | solution.py:115
  10.0 115.7 %all-gather.18.cloned.1.call-start = ((), (), s32[]{:S(2)}) async-start(), calls=%async_computation.11 | async-start | bytes 5898240 | tf_op jit(solution)/shard_map/all_gather | solution.py:150
  10.6 3.2 copy-start.23
  10.6 4.4 copy-start.29
  10.6 4.7 copy-start.30
  10.6 13.6 %copy-start = (bf16[512,768]{1,0:T(8,128)(2,1)S(1)}, bf16[512,768]{1,0:T(8,128)(2,1)}, u32[]{:S(2)}) copy-start(bf16[512,768]{1,0:T(8,128)(2,1)} %param.18) | copy-start | bytes 2359300
  10.6 153.9 %all-gather.20.cloned.1.call-start = ((), (), s32[]{:S(2)}) async-start(), calls=%async_computation.12 | async-start | bytes 5898240 | tf_op jit(solution)/shard_map/all_gather | solution.py:151
  11.2 13.8 %copy-start.24 = (s32[512]{0:T(512)S(1)}, s32[512]{0:T(512)}, u32[]{:S(2)}) copy-start(s32[512]{0:T(512)} %param.22) | copy-start | bytes 6148
  11.2 192.4 %all-gather.22.cloned.1.call-start = ((), (), s32[]{:S(2)}) async-start(), calls=%async_computation.13 | async-start | bytes 5898240 | tf_op jit(solution)/shard_map/all_gather | solution.py:152
  12.0 282.6 %reduce-scatter.8.cloned.1.call-start = ((), (), s32[]{:S(2)}) async-start(), calls=%async_computation.14 | async-start | bytes 1474560 | tf_op jit(solution)/shard_map/reduce_scatter | solution.py:299
  90.6 74.0 %copy-start.2 = (bf16[512,768]{1,0:T(8,128)(2,1)}, bf16[512,768]{1,0:T(8,128)(2,1)S(1)}, u32[]{:S(2)}) copy-start(bf16[512,768]{1,0:T(8,128)(2,1)S(1)} %multiply_convert_fusion.5) | copy-start | bytes 2359300
  132.5 71.1 %copy-start.12 = (bf16[512,768]{1,0:T(8,128)(2,1)S(1)}, bf16[512,768]{1,0:T(8,128)(2,1)}, u32[]{:S(2)}) copy-start(bf16[512,768]{1,0:T(8,128)(2,1)} %param.19) | copy-start | bytes 2359300
  214.0 7.3 copy-start.32
  214.0 7.3 copy-start.31
  214.0 7.3 copy-start.5
  214.0 7.3 copy-start.8
  264.4 54.6 %reduce-scatter.10.cloned.1.call-start = ((), (), s32[]{:S(2)}) async-start(), calls=%async_computation.15 | async-start | bytes 1474560 | tf_op jit(solution)/shard_map/reduce_scatter | solution.py:302
  267.4 79.6 %reduce-scatter.14.cloned.1.call-start = ((), (), s32[]{:S(2)}) async-start(), calls=%async_computation.17 | async-start | bytes 1474560 | tf_op jit(solution)/shard_map/reduce_scatter | solution.py:308
  270.5 105.4 %reduce-scatter.12.cloned.1.call-start = ((), (), s32[]{:S(2)}) async-start(), calls=%async_computation.16 | async-start | bytes 1474560 | tf_op jit(solution)/shard_map/reduce_scatter | solution.py:305
  270.5 3.3 copy-start.3
  273.8 152.4 %reduce-scatter.16.cloned.1.call-start = ((), (), s32[]{:S(2)}) async-start(), calls=%async_computation.18 | async-start | bytes 5898240 | tf_op jit(solution)/shard_map/reduce_scatter | solution.py:197
  280.1 196.7 %reduce-scatter.18.cloned.1.call-start = ((), (), s32[]{:S(2)}) async-start(), calls=%async_computation.19 | async-start | bytes 5898240 | tf_op jit(solution)/shard_map/reduce_scatter | solution.py:200
  286.5 240.7 %reduce-scatter.20.cloned.1.call-start = ((), (), s32[]{:S(2)}) async-start(), calls=%async_computation.20 | async-start | bytes 5898240 | tf_op jit(solution)/shard_map/reduce_scatter | solution.py:203
  294.5 286.7 %all-gather.24.cloned.1.call-start = ((), (), s32[]{:S(2)}) async-start(), calls=%async_computation.21 | async-start | bytes 2654208 | tf_op jit(solution)/shard_map/all_gather | solution.py:314
  295.1 451.2 %all-reduce.10.cloned.1.call-start = ((), (), s32[]{:S(2)}) async-start(), calls=%async_computation.22 | async-start | bytes 8847360 | tf_op jit(solution)/shard_map/psum | solution.py:317
  531.8 32.2 %copy-start.22 = (f32[512]{0:T(512)S(1)}, f32[512]{0:T(512)}, u32[]{:S(2)}) copy-start(f32[512]{0:T(512)} %get-tuple-element.221) | copy-start | bytes 6148
  564.1 3.1 copy-start.6
  564.1 3.1 copy-start.33
  746.2 3.0 copy-start.11
  (20 other events, 32.3 us)
Sparse Core Ops, SparseCore 0:
  9.5 20.1 all-gather.9
  31.3 17.5 all-gather.11
  50.4 17.4 all-gather.13
  69.3 17.4 all-gather.15
  88.2 37.4 all-gather.17
  127.1 37.4 all-gather.19
  166.1 37.4 all-gather.21
  264.5 25.6 reduce-scatter.7
  293.3 25.6 reduce-scatter.9
  321.4 25.6 reduce-scatter.13
  350.2 25.6 reduce-scatter.11
  378.2 47.9 reduce-scatter.15
  428.8 47.9 reduce-scatter.17
  479.2 47.9 reduce-scatter.19
  529.2 51.8 all-gather.23
  585.4 160.7 all-reduce.9
